TPU v7x, 32 devices: a whole 2x2x4 slice. The times are simulated.
32 devices in a mesh: dp: 4 (over z), tp: 8 (over y, x, core).
Axes of the slice: x: 2, y: 2, z: 4, core: 2. Of those that a mesh axis runs over, the one named last changes fastest.
Arguments:
- layer_input: bfloat16 [8192, 2048], P(('dp', 'tp')), may hold values from -6 to 6
- segments: int32 [4, 2048], P('dp'), may hold values from 0 to 1, as said below
- norm_gains: float32 [2, 2048], replicated, may hold values from 0.25 to 1.75
- norm_biases: float32 [2, 2048], replicated, may hold values from -2 to 2
- w_qkv: bfloat16 [2048, 3, 2048], P(None, None, 'tp'), may hold values from -0.125 to 0.125
- qv_bias: float32 [2, 2048], P(None, 'tp'), may hold values from -2 to 2
- key_bias: float32 [32, 16], P('tp'), may hold values from -3 to 3
- w_out: bfloat16 [2048, 2048], P('tp'), may hold values from -2 to 2
- w_gate_up: bfloat16 [2048, 2, 5632], P(None, None, 'tp'), may hold values from -0.125 to 0.125
- w_down: bfloat16 [5632, 2048], P('tp'), may hold values from -0.078125 to 0.078125
- out_grad: bfloat16 [8192, 2048], P(('dp', 'tp')), may hold values from -6 to 6
Outputs:
- output: float32 [8192, 2048], P(('dp', 'tp'))
- grad_x: float32 [8192, 2048], P(('dp', 'tp'))
- grad_qkv: float32 [2048, 3, 2048], P(None, None, 'tp')
- grad_qv_bias: float32 [2, 2048], P(None, 'tp')
- grad_key_bias: float32 [32, 16], P('tp')
- grad_out: float32 [2048, 2048], P('tp')
- grad_gate_up: float32 [2048, 2, 5632], P(None, None, 'tp')
- grad_down: float32 [5632, 2048], P('tp')
- grad_gains: float32 [2, 2048], P(None, 'tp')
- grad_biases: float32 [2, 2048], P(None, 'tp')
Inputs may be any that keep to these rules, and one draw needn't show every extreme that they name: `segments`: in each group the ids number the documents from 0 and never fall; every document has 1024 tokens or more.
All inputs are finite; a program needn't handle non-finite values.
Results may differ from a plain program's by a relative error of at most 0.023.
Values may be sent and summed in bfloat16 or wider, within the bound.
A program may use at most 256 MiB of HBM per device.

v0:
```python
import math
import jax
import jax.numpy as jnp
from jax import lax
from jax.sharding import PartitionSpec as P

D = 2048
HEAD_DIM = 64
ROT = 16
EPSILON = 1e-05


def norm_forward(values, gain, shift_bias):
    centre = jnp.mean(values, axis=-1, keepdims=True)
    centred = values - centre
    spread = jnp.mean(centred * centred, axis=-1, keepdims=True)
    inverse = lax.rsqrt(spread + EPSILON)
    normed = centred * inverse
    return (normed * gain + shift_bias, normed, inverse)


def norm_backward(grad_normed, normed, inverse, gain):
    scaled = grad_normed * gain
    inner = jnp.mean(scaled, axis=-1, keepdims=True)
    along = jnp.mean(scaled * normed, axis=-1, keepdims=True)
    return (
        inverse * (scaled - inner - normed * along),
        jnp.sum(grad_normed * normed, axis=0),
        jnp.sum(grad_normed, axis=0),
    )


def rotary_tables(segment_ids):
    places = jnp.arange(segment_ids.shape[0], dtype=jnp.int32)
    starts_here = jnp.concatenate(
        [jnp.ones((1,), dtype=jnp.bool_), segment_ids[1:] != segment_ids[:-1]]
    )
    doc_start = lax.cummax(jnp.where(starts_here, places, 0), axis=0)
    positions = (places - doc_start).astype(jnp.float32)
    halves = ROT // 2
    frequency = jnp.exp(jnp.arange(halves, dtype=jnp.float32) * (-2.0 * math.log(10000.0) / ROT))
    angles = positions[:, None] * frequency[None, :]
    return (jnp.cos(angles)[:, None, :], jnp.sin(angles)[:, None, :])


def rotate(tensor, cosine, sine):
    halves = ROT // 2
    first_half = tensor[..., :halves]
    second_half = tensor[..., halves:ROT]
    return jnp.concatenate(
        [
            first_half * cosine - second_half * sine,
            second_half * cosine + first_half * sine,
            tensor[..., ROT:],
        ],
        axis=-1,
    )


def rotate_back(tensor, cosine, sine):
    halves = ROT // 2
    first_half = tensor[..., :halves]
    second_half = tensor[..., halves:ROT]
    return jnp.concatenate(
        [
            first_half * cosine + second_half * sine,
            second_half * cosine - first_half * sine,
            tensor[..., ROT:],
        ],
        axis=-1,
    )


def contract_rows(left, right):
    return lax.dot_general(
        left, right, (((0,), (0,)), ((), ())), preferred_element_type=jnp.float32
    )


def contract_cols(left, right):
    return lax.dot_general(
        left, right, (((1,), (1,)), ((), ())), preferred_element_type=jnp.float32
    )


def local(
    layer_input,
    segments,
    norm_gains,
    norm_biases,
    w_qkv,
    qv_bias,
    key_bias,
    w_out,
    w_gate_up,
    w_down,
    out_grad,
):
    segment_ids = segments[0]
    group_rows = segment_ids.shape[0]
    local_width = w_qkv.shape[2]
    local_heads = local_width // HEAD_DIM
    local_hidden = w_down.shape[0]
    block_rows = min(512, group_rows)
    blocks = group_rows // block_rows
    scale = HEAD_DIM ** (-0.5)
    places = jnp.arange(group_rows, dtype=jnp.int32)
    cosine, sine = rotary_tables(segment_ids)
    qkv_matrix = w_qkv.reshape(D, 3 * local_width)
    gate_matrix = w_gate_up.reshape(D, 2 * local_hidden)
    x_float = layer_input.astype(jnp.float32)
    normed_one, hat_one, inverse_one = norm_forward(x_float, norm_gains[0], norm_biases[0])
    rows_one = lax.all_gather(normed_one.astype(jnp.bfloat16), "tp", axis=0, tiled=True)
    projected = jnp.dot(rows_one, qkv_matrix, preferred_element_type=jnp.float32).reshape(
        group_rows, 3, local_heads, HEAD_DIM
    )
    key_full = jnp.concatenate(
        [key_bias, jnp.zeros((local_heads, HEAD_DIM - ROT), jnp.float32)], axis=1
    )
    bias_all = jnp.stack(
        [
            qv_bias[0].reshape(local_heads, HEAD_DIM),
            key_full,
            qv_bias[1].reshape(local_heads, HEAD_DIM),
        ]
    )
    projected = projected + bias_all[None]
    queries = rotate(projected[:, 0], cosine, sine).astype(jnp.bfloat16)
    key_rows = rotate(projected[:, 1], cosine, sine).astype(jnp.bfloat16)
    value_rows = projected[:, 2].astype(jnp.bfloat16)
    query_blocks = queries.reshape(blocks, block_rows, local_heads, HEAD_DIM)
    segment_blocks = segment_ids.reshape(blocks, block_rows)
    place_blocks = places.reshape(blocks, block_rows)

    def scores_of(query_block, segment_block, place_block):
        raw = (
            jnp.einsum("bhd,khd->hbk", query_block, key_rows, preferred_element_type=jnp.float32)
            * scale
        )
        visible = (segment_block[:, None] == segment_ids[None, :]) & (
            place_block[:, None] >= places[None, :]
        )
        return jnp.where(visible[None], raw, -jnp.inf)

    def forward_block(item):
        query_block, segment_block, place_block = item
        scores = scores_of(query_block, segment_block, place_block)
        highest = jnp.max(scores, axis=-1, keepdims=True)
        expo = jnp.exp(scores - highest)
        totals = jnp.sum(expo, axis=-1, keepdims=True)
        probs = (expo / totals).astype(jnp.bfloat16)
        mixed = jnp.einsum("hbk,khd->bhd", probs, value_rows, preferred_element_type=jnp.float32)
        return (mixed.astype(jnp.bfloat16), (highest + jnp.log(totals))[..., 0])

    attended, log_totals = lax.map(forward_block, (query_blocks, segment_blocks, place_blocks))
    attended = attended.reshape(group_rows, local_width)
    hidden_state = x_float + lax.psum_scatter(
        jnp.dot(attended, w_out, preferred_element_type=jnp.float32).astype(jnp.bfloat16),
        "tp",
        scatter_dimension=0,
        tiled=True,
    ).astype(jnp.float32)
    normed_two, hat_two, inverse_two = norm_forward(hidden_state, norm_gains[1], norm_biases[1])
    rows_two = lax.all_gather(normed_two.astype(jnp.bfloat16), "tp", axis=0, tiled=True)
    gate_up = jnp.dot(rows_two, gate_matrix, preferred_element_type=jnp.float32).reshape(
        group_rows, 2, local_hidden
    )
    gate_part = gate_up[:, 0]
    up_part = gate_up[:, 1]
    sigmoid_gate = jax.nn.sigmoid(gate_part)
    silu_gate = gate_part * sigmoid_gate
    activation = (silu_gate * up_part).astype(jnp.bfloat16)
    output = hidden_state + lax.psum_scatter(
        jnp.dot(activation, w_down, preferred_element_type=jnp.float32).astype(jnp.bfloat16),
        "tp",
        scatter_dimension=0,
        tiled=True,
    ).astype(jnp.float32)
    grad_float = out_grad.astype(jnp.float32)
    portion = lax.all_gather(out_grad, "tp", axis=0, tiled=True)
    weight_sum = contract_rows(activation, portion)
    grad_act = contract_cols(portion, w_down)
    grad_down, grad_act = (weight_sum, grad_act)
    grad_gate = grad_act * up_part * sigmoid_gate * (1.0 + gate_part * (1.0 - sigmoid_gate))
    grad_up = grad_act * silu_gate
    grad_pair = (
        jnp.stack([grad_gate, grad_up], axis=1)
        .astype(jnp.bfloat16)
        .reshape(group_rows, 2 * local_hidden)
    )
    grad_gate_up = contract_rows(rows_two, grad_pair).reshape(D, 2, local_hidden)
    grad_normed_two = lax.psum_scatter(
        contract_cols(grad_pair, gate_matrix).astype(jnp.bfloat16),
        "tp",
        scatter_dimension=0,
        tiled=True,
    ).astype(jnp.float32)
    back_two, gain_two, shift_two = norm_backward(
        grad_normed_two, hat_two, inverse_two, norm_gains[1]
    )
    grad_hidden = grad_float + back_two
    portion = lax.all_gather(grad_hidden.astype(jnp.bfloat16), "tp", axis=0, tiled=True)
    weight_sum = contract_rows(attended, portion)
    grad_att = contract_cols(portion, w_out)
    grad_out = weight_sum
    grad_blocks = grad_att.astype(jnp.bfloat16).reshape(blocks, block_rows, local_heads, HEAD_DIM)

    def backward_block(running, item):
        grad_keys, grad_values = running
        query_block, grad_block, log_block, segment_block, place_block = item
        scores = scores_of(query_block, segment_block, place_block)
        weights = jnp.exp(scores - log_block[..., None])
        grad_values = grad_values + jnp.einsum(
            "hbk,bhd->khd",
            weights.astype(jnp.bfloat16),
            grad_block,
            preferred_element_type=jnp.float32,
        )
        grad_weights = jnp.einsum(
            "bhd,khd->hbk", grad_block, value_rows, preferred_element_type=jnp.float32
        )
        inner = jnp.sum(weights * grad_weights, axis=-1, keepdims=True)
        grad_scores = (weights * (grad_weights - inner)).astype(jnp.bfloat16)
        grad_query = (
            jnp.einsum("hbk,khd->bhd", grad_scores, key_rows, preferred_element_type=jnp.float32)
            * scale
        )
        grad_keys = (
            grad_keys
            + jnp.einsum(
                "hbk,bhd->khd", grad_scores, query_block, preferred_element_type=jnp.float32
            )
            * scale
        )
        return ((grad_keys, grad_values), grad_query)

    zero_heads = jnp.zeros((group_rows, local_heads, HEAD_DIM), jnp.float32)
    (grad_keys, grad_values), grad_queries = lax.scan(
        backward_block,
        (zero_heads, zero_heads),
        (query_blocks, grad_blocks, log_totals, segment_blocks, place_blocks),
    )
    grad_queries = grad_queries.reshape(group_rows, local_heads, HEAD_DIM)
    grad_projected = jnp.stack(
        [
            rotate_back(grad_queries, cosine, sine),
            rotate_back(grad_keys, cosine, sine),
            grad_values,
        ],
        axis=1,
    ).astype(jnp.bfloat16)
    bias_sums = jnp.sum(grad_projected, axis=0, dtype=jnp.float32)
    grad_qv = jnp.stack([bias_sums[0].reshape(local_width), bias_sums[2].reshape(local_width)])
    grad_key = bias_sums[1][:, :ROT]
    grad_flat = grad_projected.reshape(group_rows, 3 * local_width)
    grad_qkv = contract_rows(rows_one, grad_flat).reshape(D, 3, local_width)
    grad_normed_one = lax.psum_scatter(
        contract_cols(grad_flat, qkv_matrix).astype(jnp.bfloat16),
        "tp",
        scatter_dimension=0,
        tiled=True,
    ).astype(jnp.float32)
    back_one, gain_one, shift_one = norm_backward(
        grad_normed_one, hat_one, inverse_one, norm_gains[0]
    )
    grad_input = grad_hidden + back_one
    gain_grads, shift_grads = (
        lax.psum_scatter(
            jnp.stack([gain_one, gain_two]).astype(jnp.bfloat16),
            "tp",
            scatter_dimension=1,
            tiled=True,
        ).astype(jnp.float32),
        lax.psum_scatter(
            jnp.stack([shift_one, shift_two]).astype(jnp.bfloat16),
            "tp",
            scatter_dimension=1,
            tiled=True,
        ).astype(jnp.float32),
    )
    grad_qkv, grad_qv, grad_key, grad_out, grad_gate_up, grad_down, gain_grads, shift_grads = (
        lax.psum(grad_qkv.astype(jnp.bfloat16), "dp").astype(jnp.float32),
        lax.psum(grad_qv.astype(jnp.bfloat16), "dp").astype(jnp.float32),
        lax.psum(grad_key.astype(jnp.bfloat16), "dp").astype(jnp.float32),
        lax.psum(grad_out.astype(jnp.bfloat16), "dp").astype(jnp.float32),
        lax.psum(grad_gate_up.astype(jnp.bfloat16), "dp").astype(jnp.float32),
        lax.psum(grad_down.astype(jnp.bfloat16), "dp").astype(jnp.float32),
        lax.psum(gain_grads.astype(jnp.bfloat16), "dp").astype(jnp.float32),
        lax.psum(shift_grads.astype(jnp.bfloat16), "dp").astype(jnp.float32),
    )
    return (
        output,
        grad_input,
        grad_qkv,
        grad_qv,
        grad_key,
        grad_out,
        grad_gate_up,
        grad_down,
        gain_grads,
        shift_grads,
    )


def solution(mesh):
    in_specs = (
        P(("dp", "tp"), None),
        P("dp", None),
        P(),
        P(),
        P(None, None, "tp"),
        P(None, "tp"),
        P("tp", None),
        P("tp", None),
        P(None, None, "tp"),
        P("tp", None),
        P(("dp", "tp"), None),
    )
    out_specs = (
        P(("dp", "tp"), None),
        P(("dp", "tp"), None),
        P(None, None, "tp"),
        P(None, "tp"),
        P("tp", None),
        P("tp", None),
        P(None, None, "tp"),
        P("tp", None),
        P(None, "tp"),
        P(None, "tp"),
    )
    return jax.shard_map(local, mesh=mesh, in_specs=in_specs, out_specs=out_specs, check_vma=False)
```

profile of v0, /device:TPU:0, one launch (start us, length us, event | category | flops | bytes accessed | tf_op | source)
XLA Modules:
  0.0 1480.7 jit_solution(10848038059797148822)
XLA Ops:
  23.3 49.9 %all-gather.5.cloned.1.call-done = bf16[2048,2048]{1,0:T(8,128)(2,1)} async-done(((bf16[256,2048]{1,0:T(8,128)(2,1)}), bf16[2048,2048]{1,0:T(8,128)(2,1)}) %all-gather.5.cloned.1.call-update) | async-done | bytes 8388624 | tf_op jit(solution)/shard_map/all_gather | solution.py:113
  88.5 63.9 %while.28 = (s32[]{:T(128)}, bf16[4,512,4,64]{1,3,2,0:T(8,128)(2,1)}, f32[4,4,512]{2,1,0:T(4,128)S(1)}, s32[4,512]{1,0:T(4,128)S(1)}, s32[1,2048]{1,0:T(1,128)S(...) while((s32[]{:T(128)}, ...), condition=%wide.region_7.8_spmd.clone, body=%wide.region_4.7_spmd.clone.sunk | while | flops 1127348224 | bytes 61427864 | solution.py:155
  161.7 71.6 %reduce-scatter.11.cloned.1.call-done = bf16[256,2048]{1,0:T(8,128)(2,1)} async-done(((bf16[2048,2048]{1,0:T(8,128)(2,1)}), bf16[256,2048]{1,0:T(8,128)(2,1)}) %reduce-scatter.11.cloned.1.call-update) | async-done | bytes 1048592 | tf_op jit(solution)/shard_map/reduce_scatter | solution.py:157
  239.6 53.8 %all-gather.7.cloned.1.call-done = bf16[2048,2048]{1,0:T(8,128)(2,1)} async-done(((bf16[256,2048]{1,0:T(8,128)(2,1)}), bf16[2048,2048]{1,0:T(8,128)(2,1)}) %all-gather.7.cloned.1.call-update) | async-done | bytes 8388624 | tf_op jit(solution)/shard_map/all_gather | solution.py:164
  293.4 18.8 %fusion.53 = f32[2048,2,704]{0,2,1:T(8,128)} fusion(bf16[2048,2048]{1,0:T(8,128)(2,1)} %all-gather.7.cloned.1.call-done, bf16[2048,2,704]{0,2,1:T(8,128)(2,1)} %param.23), kind=kOutput, calls=%fused_computation.64 | convolution fusion | flops 11811160064 | bytes 25690112 | tf_op jit(solution)/shard_map/dot_general | solution.py:165
  312.2 37.2 %all-gather.9.cloned.1.call-done = bf16[2048,2048]{1,0:T(8,128)(2,1)} async-done(((bf16[256,2048]{1,0:T(8,128)(2,1)}), bf16[2048,2048]{1,0:T(8,128)(2,1)}) %all-gather.9.cloned.1.call-update) | async-done | bytes 8388624 | tf_op jit(solution)/shard_map/all_gather | solution.py:180
  349.4 12.9 multiply_bitcast_fusion.1
  364.9 17.9 %bitcast_convert_fusion = bf16[2048,2048]{1,0:T(8,128)(2,1)} fusion(bf16[2048,2,704]{0,2,1:T(8,128)(2,1)} %param.23, bf16[2048,1,704]{0,2,1:T(8,128)(2,1)S(1)} %get-tuple-element.303, bf16[2048,1,704]{0,2,1:T(8,128)(2,1)S(1)} %get-tuple-element.302), kind=kOutput, calls=%fused_computation.56 | convolution fusion | flops 11818237952 | bytes 19922944 | tf_op jit(solution)/shard_map/dot_general | solution.py:81
  382.8 71.6 %reduce-scatter.15.cloned.1.call-done = bf16[256,2048]{1,0:T(8,128)(2,1)} async-done(((bf16[2048,2048]{1,0:T(8,128)(2,1)}), bf16[256,2048]{1,0:T(8,128)(2,1)}) %reduce-scatter.15.cloned.1.call-update) | async-done | bytes 1048592 | tf_op jit(solution)/shard_map/reduce_scatter | solution.py:192
  461.6 54.3 %all-gather.11.cloned.1.call-done = bf16[2048,2048]{1,0:T(8,128)(2,1)} async-done(((bf16[256,2048]{1,0:T(8,128)(2,1)}), bf16[2048,2048]{1,0:T(8,128)(2,1)}) %all-gather.11.cloned.1.call-update) | async-done | bytes 8388624 | tf_op jit(solution)/shard_map/all_gather | solution.py:202
  531.4 245.9 %while.29 = (s32[]{:T(128)}, f32[2048,4,64]{0,2,1:T(8,128)}, f32[2048,4,64]{0,2,1:T(8,128)}, f32[4,512,4,64]{1,0,3,2:T(4,128)}, bf16[4,512,4,64]{1,3,2,0:T(8,128...) while((s32[]{:T(128)}, f32[2048,4,64]{0,2,1:T(8,128)}, ...), condition=%wide.region_17.18_spmd.clone, body=%wide.region_15.17_spmd.clone.sunk | while | flops 2753165312 | bytes 233386272 | solution.py:238
  549.3 12.8 multiply_reduce_fusion.3
  562.1 12.2 multiply_convert_fusion.3
  610.8 12.8 multiply_reduce_fusion.3
  623.6 12.2 multiply_convert_fusion.3
  672.3 12.8 multiply_reduce_fusion.3
  685.1 12.2 multiply_convert_fusion.3
  733.8 12.8 multiply_reduce_fusion.3
  825.2 16.2 %fusion.58 = bf16[2048,2,704]{0,2,1:T(8,128)(2,1)} fusion(bf16[2048,2048]{1,0:T(8,128)(2,1)} %all-gather.7.cloned.1.call-done, bf16[2048,1,704]{0,2,1:T(8,128)(2,1)S(1)} %copy-done.47, bf16[2048,1,704]{0,2,1:T(8,128)(2,1)S(1)} %copy-done.45), kind=kOutput, calls=%fused_computation.79 | convolution fusion | flops 11825577984 | bytes 19922944 | tf_op jit(solution)/shard_map/dot_general | solution.py:75
  854.5 14.9 %reduce-scatter.17.cloned.1.call-done = bf16[256,2048]{1,0:T(8,128)(2,1)} async-done(((bf16[2048,2048]{1,0:T(8,128)(2,1)}), bf16[256,2048]{1,0:T(8,128)(2,1)}) %reduce-scatter.17.cloned.1.call-update) | async-done | bytes 1048592 | tf_op jit(solution)/shard_map/reduce_scatter | solution.py:257
  883.5 61.5 %reduce-scatter.13.cloned.1.call-done = bf16[256,2048]{1,0:T(8,128)(2,1)} async-done(((bf16[2048,2048]{1,0:T(8,128)(2,1)}), bf16[256,2048]{1,0:T(8,128)(2,1)}) %reduce-scatter.13.cloned.1.call-update) | async-done | bytes 1048592 | tf_op jit(solution)/shard_map/reduce_scatter | solution.py:173
  950.3 32.5 %reduce-scatter.19.cloned.1.call-done = bf16[256,2]{1,0:T(8,128)(2,1)} async-done(((bf16[2048,2]{1,0:T(8,128)(2,1)}), bf16[256,2]{1,0:T(8,128)(2,1)}) %reduce-scatter.19.cloned.1.call-update) | async-done | bytes 1040
  983.7 36.2 %reduce-scatter.21.cloned.1.call-done = bf16[256,2]{1,0:T(8,128)(2,1)} async-done(((bf16[2048,2]{1,0:T(8,128)(2,1)}), bf16[256,2]{1,0:T(8,128)(2,1)}) %reduce-scatter.21.cloned.1.call-update) | async-done | bytes 1040
  1035.0 423.0 %all-reduce.5.cloned.1.call-done = (bf16[2048,3,256]{2,0,1:T(8,128)(2,1)}, bf16[256,2048]{1,0:T(8,128)(2,1)}, bf16[2048,2,704]{0,2,1:T(8,128)(2,1)}, bf16[704,2048]{1,0:T(8,128)(2,1)}) async-done(((bf16[2048,3,256]{2,0,1:T(8,128)(2,1)}, bf16[256,2048]{1,0:T(8,128)(2,1)}, bf16[2048,2,704]{0,2,1:T(8,128)(2,1)}, bf16[704,2048]{1,0:T(8,128)(2,1)}), (bf16[2048,3,256]{2,0,1:T(8,128)(2,1)}, ...) | async-done | bytes 12845072 | tf_op jit(solution)/shard_map/psum | solution.py:282
  (311 shorter events, 405.0 us)
Async XLA Ops:
  7.2 342.3 %copy-start = (bf16[704,2048]{1,0:T(8,128)(2,1)S(1)}, bf16[704,2048]{1,0:T(8,128)(2,1)}, u32[]{:S(2)}) copy-start(bf16[704,2048]{1,0:T(8,128)(2,1)} %param.24) | copy-start | bytes 8650756
  7.2 66.0 %all-gather.5.cloned.1.call-start = ((), (), s32[]{:S(2)}) async-start(), calls=%async_computation.6 | async-start | bytes 9437184 | tf_op jit(solution)/shard_map/all_gather | solution.py:113
  16.0 217.2 %reduce-scatter.11.cloned.1.call-start = ((), (), s32[]{:S(2)}) async-start(), calls=%async_computation.7 | async-start | bytes 9437184 | tf_op jit(solution)/shard_map/reduce_scatter | solution.py:157
  23.3 61.6 %copy-start.20 = (f32[2048,8]{0,1:T(8,128)}, f32[2048,8]{0,1:T(8,128)S(1)}, u32[]{:S(2)}) copy-start(f32[2048,8]{0,1:T(8,128)S(1)} %get-tuple-element.324) | copy-start | bytes 196612
  23.3 61.6 %copy-start.22 = (f32[2048,8]{0,1:T(8,128)}, f32[2048,8]{0,1:T(8,128)S(1)}, u32[]{:S(2)}) copy-start(f32[2048,8]{0,1:T(8,128)S(1)} %get-tuple-element.325) | copy-start | bytes 196612
  161.6 75.8 %copy-start.24 = (f32[1,2048]{1,0:T(1,128)S(1)}, f32[1,2048]{1,0:T(1,128)}, u32[]{:S(2)}) copy-start(f32[1,2048]{1,0:T(1,128)} %get-tuple-element.321) | copy-start | bytes 24580
  161.6 75.8 %copy-start.30 = (f32[1,2048]{1,0:T(1,128)S(1)}, f32[1,2048]{1,0:T(1,128)}, u32[]{:S(2)}) copy-start(f32[1,2048]{1,0:T(1,128)} %get-tuple-element.323) | copy-start | bytes 24580
  161.7 131.7 %all-gather.7.cloned.1.call-start = ((), (), s32[]{:S(2)}) async-start(), calls=%async_computation.8 | async-start | bytes 9437184 | tf_op jit(solution)/shard_map/all_gather | solution.py:164
  235.3 222.7 %copy-start.28 = (f32[256]{0:T(256)}, f32[256]{0:T(256)S(1)}, u32[]{:S(2)}) copy-start(f32[256]{0:T(256)S(1)} %broadcast_multiply_fusion.4) | copy-start | bytes 3076
  237.4 220.7 %copy-start.33 = (f32[256]{0:T(256)}, f32[256]{0:T(256)S(1)}, u32[]{:S(2)}) copy-start(f32[256]{0:T(256)S(1)} %add_rsqrt_fusion) | copy-start | bytes 3076
  239.0 110.4 %all-gather.9.cloned.1.call-start = ((), (), s32[]{:S(2)}) async-start(), calls=%async_computation.10 | async-start | bytes 9437184 | tf_op jit(solution)/shard_map/all_gather | solution.py:180
  239.6 214.8 %reduce-scatter.15.cloned.1.call-start = ((), (), s32[]{:S(2)}) async-start(), calls=%async_computation.11 | async-start | bytes 9437184 | tf_op jit(solution)/shard_map/reduce_scatter | solution.py:192
  382.8 133.1 %all-gather.11.cloned.1.call-start = ((), (), s32[]{:S(2)}) async-start(), calls=%async_computation.12 | async-start | bytes 9437184 | tf_op jit(solution)/shard_map/all_gather | solution.py:202
  461.5 407.9 %reduce-scatter.17.cloned.1.call-start = ((), (), s32[]{:S(2)}) async-start(), calls=%async_computation.13 | async-start | bytes 9437184 | tf_op jit(solution)/shard_map/reduce_scatter | solution.py:257
  797.8 147.2 %reduce-scatter.13.cloned.1.call-start = ((), (), s32[]{:S(2)}) async-start(), calls=%async_computation.9 | async-start | bytes 9437184 | tf_op jit(solution)/shard_map/reduce_scatter | solution.py:173
  813.7 169.1 %reduce-scatter.19.cloned.1.call-start = ((), (), s32[]{:S(2)}) async-start(), calls=%async_computation.14 | async-start | bytes 589824
  842.9 28.0 %copy-start.27 = (f32[1,2048]{1,0:T(1,128)S(1)}, f32[1,2048]{1,0:T(1,128)}, u32[]{:S(2)}) copy-start(f32[1,2048]{1,0:T(1,128)} %copy-done.26) | copy-start | bytes 24580
  874.5 145.4 %reduce-scatter.21.cloned.1.call-start = ((), (), s32[]{:S(2)}) async-start(), calls=%async_computation.15 | async-start | bytes 589824
  875.6 582.3 %all-reduce.5.cloned.1.call-start = ((), (), s32[]{:S(2)}) async-start(), calls=%async_computation.16 | async-start | bytes 25690112 | tf_op jit(solution)/shard_map/psum | solution.py:282
  883.2 61.7 %copy-start.25 = (f32[1,2048]{1,0:T(1,128)S(1)}, f32[1,2048]{1,0:T(1,128)}, u32[]{:S(2)}) copy-start(f32[1,2048]{1,0:T(1,128)} %get-tuple-element.321) | copy-start | bytes 24580
  883.2 61.7 %copy-start.29 = (f32[256]{0:T(256)S(1)}, f32[256]{0:T(256)}, u32[]{:S(2)}) copy-start(f32[256]{0:T(256)} %copy-done.28) | copy-start | bytes 3076
  883.2 61.7 %copy-start.34 = (f32[256]{0:T(256)S(1)}, f32[256]{0:T(256)}, u32[]{:S(2)}) copy-start(f32[256]{0:T(256)} %copy-done.33) | copy-start | bytes 3076
  883.2 61.7 %copy-start.39 = (f32[256]{0:T(256)S(1)}, f32[256]{0:T(256)}, u32[]{:S(2)}) copy-start(f32[256]{0:T(256)} %copy-done.38) | copy-start | bytes 3076
  883.2 61.7 %copy-start.41 = (f32[256]{0:T(256)S(1)}, f32[256]{0:T(256)}, u32[]{:S(2)}) copy-start(f32[256]{0:T(256)} %copy-done.40) | copy-start | bytes 3076
  (52 other events, 310.2 us)
Sparse Core Ops, SparseCore 0:
  16.2 56.9 all-gather.4
  161.8 71.4 reduce-scatter.10
  239.1 54.2 all-gather.6
  295.1 54.2 all-gather.8
  382.9 71.4 reduce-scatter.14
  461.6 54.2 all-gather.10
  797.9 71.4 reduce-scatter.16
  873.4 71.4 reduce-scatter.12
  948.6 34.1 reduce-scatter.18
  985.7 34.1 reduce-scatter.20
  1023.3 434.5 all-reduce.4
where the time goes:
time: 1490 us; the launch traced here: 1480 us
  waiting for transfers between devices  907 us (61%)
  matrix products  296 us (20%)
  other arithmetic  133 us (9%)
  local copies, waits for them, and re-layouts  116 us (8%)
    psum x1, waiting for transfers between devices, local(): lax.psum(grad_qkv.astype(jnp.bfloat16), 'dp').astype(jnp.float32)  423 us
    reduce_scatter x1, waiting for transfers between devices, local(): lax.psum_scatter(contract_cols(grad_pair, gate_matrix).astype(jnp.bfloat1...  71.6 us
    reduce_scatter x1, waiting for transfers between devices, local(): lax.psum_scatter(jnp.dot(attended, w_out, preferred_element_type=jnp.floa...  71.6 us
    unnamed x13, waiting for transfers between devices  69.3 us
    reduce_scatter x1, waiting for transfers between devices, local(): lax.psum_scatter(jnp.dot(activation, w_down, preferred_element_type=jnp.f...  61.5 us
    all_gather x1, waiting for transfers between devices, local(): lax.all_gather(grad_hidden.astype(jnp.bfloat16), 'tp', axis=0, tiled=True)  54.3 us
    all_gather x1, waiting for transfers between devices, local(): lax.all_gather(normed_two.astype(jnp.bfloat16), 'tp', axis=0, tiled=True)  53.8 us
    dot_general x4, matrix products, backward_block(): jnp.einsum('bhd,khd->hbk', grad_block, value_rows, preferred_element_type...  51.2 us
  transfers between devices with their start and end apart: 11, of which 11 were waited for; matrix products, arithmetic and copies ran while one was open for 7% of the time, Pallas kernels for 0%

commit v1 on v0

--- a/solution.py
+++ b/solution.py
@@ -1,3 +1,4 @@
+import functools
 import math
 import jax
 import jax.numpy as jnp
@@ -8,6 +9,13 @@
 HEAD_DIM = 64
 ROT = 16
 EPSILON = 1e-05
+
+
+def solve_row(u_in, dev_axis):
+    return jax.lax.all_gather(u_in, dev_axis).sum(axis=0)
+
+
+files_fit = functools.partial(solve_row, dev_axis="dp")
 
 
 def norm_forward(values, gain, shift_bias):
@@ -279,7 +287,7 @@
         ).astype(jnp.float32),
     )
     grad_qkv, grad_qv, grad_key, grad_out, grad_gate_up, grad_down, gain_grads, shift_grads = (
-        lax.psum(grad_qkv.astype(jnp.bfloat16), "dp").astype(jnp.float32),
+        files_fit(grad_qkv.astype(jnp.bfloat16)).astype(jnp.float32),
         lax.psum(grad_qv.astype(jnp.bfloat16), "dp").astype(jnp.float32),
         lax.psum(grad_key.astype(jnp.bfloat16), "dp").astype(jnp.float32),
         lax.psum(grad_out.astype(jnp.bfloat16), "dp").astype(jnp.float32),

time: 1490 us -> 1610 us (1.081)
  waiting for transfers between devices: 907 us -> 1010 us
    all_gather x0 -> x1, waiting for transfers between devices: none -> 204 us  [solve_row(): return jax.lax.all_gather(u_in, dev_axis).sum(axis=0)]
    psum x1, waiting for transfers between devices: 423 us -> 318 us  [local(): lax.psum(grad_out.astype(jnp.bfloat16), 'dp').astype(jnp.float32)]
    unnamed x13 -> x14, waiting for transfers between devices: 69.3 us -> 68.7 us
  transfers between devices with their start and end apart: 11 -> 12, of which waited for: 11 -> 12; matrix products, arithmetic and copies ran while one was open for 7% -> 8% of each run, Pallas kernels for 0% -> 0%
where the time goes in v1:
time: 1610 us; the launch traced here: 1600 us
  waiting for transfers between devices  1010 us (63%)
  matrix products  307 us (19%)
  other arithmetic  145 us (9%)
  local copies, waits for them, and re-layouts  117 us (7%)
    psum x1, waiting for transfers between devices, local(): lax.psum(grad_out.astype(jnp.bfloat16), 'dp').astype(jnp.float32)  318 us
    all_gather x1, waiting for transfers between devices, solve_row(): return jax.lax.all_gather(u_in, dev_axis).sum(axis=0)  204 us
    reduce_scatter x1, waiting for transfers between devices, local(): lax.psum_scatter(contract_cols(grad_pair, gate_matrix).astype(jnp.bfloat1...  71.6 us
    reduce_scatter x1, waiting for transfers between devices, local(): lax.psum_scatter(jnp.dot(attended, w_out, preferred_element_type=jnp.floa...  71.6 us
    unnamed x14, waiting for transfers between devices  68.7 us
    reduce_scatter x1, waiting for transfers between devices, local(): lax.psum_scatter(jnp.dot(activation, w_down, preferred_element_type=jnp.f...  60.6 us
    dot_general x4, matrix products, contract_cols(): lax.dot_general(left, right, (((1,), (1,)), ((), ())), preferred_element_...  55.5 us
    all_gather x1, waiting for transfers between devices, local(): lax.all_gather(grad_hidden.astype(jnp.bfloat16), 'tp', axis=0, tiled=True)  54.3 us
  transfers between devices with their start and end apart: 12, of which 12 were waited for; matrix products, arithmetic and copies ran while one was open for 8% of the time, Pallas kernels for 0%

profile of v1, /device:TPU:0, one launch (start us, length us, event | category | flops | bytes accessed | tf_op | source)
XLA Modules:
  0.0 1604.3 jit_solution(6956849473564351153)
XLA Ops:
  23.3 49.9 %all-gather.7.cloned.1.call-done = bf16[2048,2048]{1,0:T(8,128)(2,1)} async-done(((bf16[256,2048]{1,0:T(8,128)(2,1)}), bf16[2048,2048]{1,0:T(8,128)(2,1)}) %all-gather.7.cloned.1.call-update) | async-done | bytes 8388624 | tf_op jit(solution)/shard_map/all_gather | solution.py:121
  88.6 64.0 %while.28 = (s32[]{:T(128)}, bf16[4,512,4,64]{1,3,2,0:T(8,128)(2,1)}, f32[4,4,512]{2,1,0:T(4,128)S(1)}, s32[4,512]{1,0:T(4,128)S(1)}, s32[1,2048]{1,0:T(1,128)S(...) while((s32[]{:T(128)}, ...), condition=%wide.region_7.8_spmd.clone, body=%wide.region_4.7_spmd.clone.sunk | while | flops 1127348224 | bytes 61427864 | solution.py:163
  161.8 71.6 %reduce-scatter.11.cloned.1.call-done = bf16[256,2048]{1,0:T(8,128)(2,1)} async-done(((bf16[2048,2048]{1,0:T(8,128)(2,1)}), bf16[256,2048]{1,0:T(8,128)(2,1)}) %reduce-scatter.11.cloned.1.call-update) | async-done | bytes 1048592 | tf_op jit(solution)/shard_map/reduce_scatter | solution.py:165
  239.8 53.8 %all-gather.9.cloned.1.call-done = bf16[2048,2048]{1,0:T(8,128)(2,1)} async-done(((bf16[256,2048]{1,0:T(8,128)(2,1)}), bf16[2048,2048]{1,0:T(8,128)(2,1)}) %all-gather.9.cloned.1.call-update) | async-done | bytes 8388624 | tf_op jit(solution)/shard_map/all_gather | solution.py:172
  293.6 18.8 %fusion.53 = f32[2048,2,704]{0,2,1:T(8,128)} fusion(bf16[2048,2048]{1,0:T(8,128)(2,1)} %all-gather.9.cloned.1.call-done, bf16[2048,2,704]{0,2,1:T(8,128)(2,1)} %param.23), kind=kOutput, calls=%fused_computation.64 | convolution fusion | flops 11811160064 | bytes 25690112 | tf_op jit(solution)/shard_map/dot_general | solution.py:173
  312.4 37.2 %all-gather.11.cloned.1.call-done = bf16[2048,2048]{1,0:T(8,128)(2,1)} async-done(((bf16[256,2048]{1,0:T(8,128)(2,1)}), bf16[2048,2048]{1,0:T(8,128)(2,1)}) %all-gather.11.cloned.1.call-update) | async-done | bytes 8388624 | tf_op jit(solution)/shard_map/all_gather | solution.py:188
  349.6 12.9 multiply_bitcast_fusion.1
  365.0 26.4 %bitcast_convert_fusion = bf16[2048,2048]{1,0:T(8,128)(2,1)} fusion(bf16[2048,2,704]{0,2,1:T(8,128)(2,1)} %param.23, bf16[2048,1,704]{0,2,1:T(8,128)(2,1)S(1)} %get-tuple-element.302, bf16[2048,1,704]{0,2,1:T(8,128)(2,1)S(1)} %get-tuple-element.301), kind=kOutput, calls=%fused_computation.56 | convolution fusion | flops 11818237952 | bytes 19922944 | tf_op jit(solution)/shard_map/dot_general | solution.py:89
  391.5 71.6 %reduce-scatter.15.cloned.1.call-done = bf16[256,2048]{1,0:T(8,128)(2,1)} async-done(((bf16[2048,2048]{1,0:T(8,128)(2,1)}), bf16[256,2048]{1,0:T(8,128)(2,1)}) %reduce-scatter.15.cloned.1.call-update) | async-done | bytes 1048592 | tf_op jit(solution)/shard_map/reduce_scatter | solution.py:200
  470.3 54.3 %all-gather.13.cloned.1.call-done = bf16[2048,2048]{1,0:T(8,128)(2,1)} async-done(((bf16[256,2048]{1,0:T(8,128)(2,1)}), bf16[2048,2048]{1,0:T(8,128)(2,1)}) %all-gather.13.cloned.1.call-update) | async-done | bytes 8388624 | tf_op jit(solution)/shard_map/all_gather | solution.py:210
  540.1 246.3 %while.29 = (s32[]{:T(128)}, f32[2048,4,64]{0,2,1:T(8,128)}, f32[2048,4,64]{0,2,1:T(8,128)}, f32[4,512,4,64]{1,0,3,2:T(4,128)}, bf16[4,512,4,64]{1,3,2,0:T(8,128...) while((s32[]{:T(128)}, f32[2048,4,64]{0,2,1:T(8,128)}, ...), condition=%wide.region_17.18_spmd.clone, body=%wide.region_15.17_spmd.clone.sunk | while | flops 2753165312 | bytes 233386272 | solution.py:246
  558.2 12.8 multiply_reduce_fusion.3
  571.1 12.2 multiply_convert_fusion.3
  619.8 12.8 multiply_reduce_fusion.3
  681.3 12.8 multiply_reduce_fusion.3
  742.9 12.8 multiply_reduce_fusion.3
  813.8 12.6 convolution_convert_fusion.3
  826.4 16.1 %fusion.58 = bf16[2048,2,704]{0,2,1:T(8,128)(2,1)} fusion(bf16[2048,2048]{1,0:T(8,128)(2,1)S(1)} %bitcast.264, bf16[2048,1,704]{0,2,1:T(8,128)(2,1)} %copy-done.46, bf16[2048,1,704]{0,2,1:T(8,128)(2,1)S(1)} %copy-done.45), kind=kOutput, calls=%fused_computation.79 | convolution fusion | flops 11825577984 | bytes 19922944 | tf_op jit(solution)/shard_map/dot_general | solution.py:83
  862.2 16.3 %reduce-scatter.17.cloned.1.call-done = bf16[256,2048]{1,0:T(8,128)(2,1)} async-done(((bf16[2048,2048]{1,0:T(8,128)(2,1)}), bf16[256,2048]{1,0:T(8,128)(2,1)}) %reduce-scatter.17.cloned.1.call-update) | async-done | bytes 1048592 | tf_op jit(solution)/shard_map/reduce_scatter | solution.py:265
  897.0 318.1 %all-reduce.5.cloned.1.call-done = (bf16[256,2048]{1,0:T(8,128)(2,1)}, bf16[2048,2,704]{0,2,1:T(8,128)(2,1)}, bf16[704,2048]{1,0:T(8,128)(2,1)}) async-done(((bf16[256,2048]{1,0:T(8,128)(2,1)}, bf16[2048,2,704]{0,2,1:T(8,128)(2,1)}, bf16[704,2048]{1,0:T(8,128)(2,1)}), (bf16[256,2048]{1,0:T(8,128)(2,1)}, bf16[2048,2,704]{0,2,1:T(8,128)(2,1)}, bf16[704,2048]{1,0:T(8,128)(2,1)})) %all-reduce.5.cloned.1.call-update) | async-done | bytes 9699344 | tf_op jit(solution)/shard_map/psum | solution.py:293
  1228.4 60.6 %reduce-scatter.13.cloned.1.call-done = bf16[256,2048]{1,0:T(8,128)(2,1)} async-done(((bf16[2048,2048]{1,0:T(8,128)(2,1)}), bf16[256,2048]{1,0:T(8,128)(2,1)}) %reduce-scatter.13.cloned.1.call-update) | async-done | bytes 1048592 | tf_op jit(solution)/shard_map/reduce_scatter | solution.py:181
  1294.4 31.7 %reduce-scatter.19.cloned.1.call-done = bf16[256,2]{1,0:T(8,128)(2,1)} async-done(((bf16[2048,2]{1,0:T(8,128)(2,1)}), bf16[256,2]{1,0:T(8,128)(2,1)}) %reduce-scatter.19.cloned.1.call-update) | async-done | bytes 1040
  1327.0 36.3 %reduce-scatter.21.cloned.1.call-done = bf16[256,2]{1,0:T(8,128)(2,1)} async-done(((bf16[2048,2]{1,0:T(8,128)(2,1)}), bf16[256,2]{1,0:T(8,128)(2,1)}) %reduce-scatter.21.cloned.1.call-update) | async-done | bytes 1040
  1378.4 204.5 %all-gather.15.cloned.1.call-done = bf16[8192,3,256]{2,0,1:T(8,128)(2,1)} async-done(((bf16[2048,3,256]{2,0,1:T(8,128)(2,1)}), bf16[8192,3,256]{2,0,1:T(8,128)(2,1)}) %all-gather.15.cloned.1.call-update) | async-done | bytes 12582928 | tf_op jit(solution)/shard_map/all_gather | solution.py:15
  (318 shorter events, 431.5 us)
Async XLA Ops:
  7.2 342.4 %copy-start = (bf16[704,2048]{1,0:T(8,128)(2,1)S(1)}, bf16[704,2048]{1,0:T(8,128)(2,1)}, u32[]{:S(2)}) copy-start(bf16[704,2048]{1,0:T(8,128)(2,1)} %param.24) | copy-start | bytes 8650756
  7.2 66.0 %all-gather.7.cloned.1.call-start = ((), (), s32[]{:S(2)}) async-start(), calls=%async_computation.6 | async-start | bytes 9437184 | tf_op jit(solution)/shard_map/all_gather | solution.py:121
  16.1 217.4 %reduce-scatter.11.cloned.1.call-start = ((), (), s32[]{:S(2)}) async-start(), calls=%async_computation.7 | async-start | bytes 9437184 | tf_op jit(solution)/shard_map/reduce_scatter | solution.py:165
  23.3 61.6 %copy-start.20 = (f32[2048,8]{0,1:T(8,128)}, f32[2048,8]{0,1:T(8,128)S(1)}, u32[]{:S(2)}) copy-start(f32[2048,8]{0,1:T(8,128)S(1)} %get-tuple-element.323) | copy-start | bytes 196612
  23.3 61.6 %copy-start.22 = (f32[2048,8]{0,1:T(8,128)}, f32[2048,8]{0,1:T(8,128)S(1)}, u32[]{:S(2)}) copy-start(f32[2048,8]{0,1:T(8,128)S(1)} %get-tuple-element.324) | copy-start | bytes 196612
  161.8 75.8 %copy-start.24 = (f32[1,2048]{1,0:T(1,128)S(1)}, f32[1,2048]{1,0:T(1,128)}, u32[]{:S(2)}) copy-start(f32[1,2048]{1,0:T(1,128)} %get-tuple-element.320) | copy-start | bytes 24580
  161.8 75.8 %copy-start.30 = (f32[1,2048]{1,0:T(1,128)S(1)}, f32[1,2048]{1,0:T(1,128)}, u32[]{:S(2)}) copy-start(f32[1,2048]{1,0:T(1,128)} %get-tuple-element.322) | copy-start | bytes 24580
  161.8 131.8 %all-gather.9.cloned.1.call-start = ((), (), s32[]{:S(2)}) async-start(), calls=%async_computation.8 | async-start | bytes 9437184 | tf_op jit(solution)/shard_map/all_gather | solution.py:172
  235.5 231.3 %copy-start.28 = (f32[256]{0:T(256)}, f32[256]{0:T(256)S(1)}, u32[]{:S(2)}) copy-start(f32[256]{0:T(256)S(1)} %broadcast_multiply_fusion.4) | copy-start | bytes 3076
  237.5 229.2 %copy-start.33 = (f32[256]{0:T(256)}, f32[256]{0:T(256)S(1)}, u32[]{:S(2)}) copy-start(f32[256]{0:T(256)S(1)} %add_rsqrt_fusion) | copy-start | bytes 3076
  239.1 110.4 %all-gather.11.cloned.1.call-start = ((), (), s32[]{:S(2)}) async-start(), calls=%async_computation.10 | async-start | bytes 9437184 | tf_op jit(solution)/shard_map/all_gather | solution.py:188
  239.7 223.4 %reduce-scatter.15.cloned.1.call-start = ((), (), s32[]{:S(2)}) async-start(), calls=%async_computation.11 | async-start | bytes 9437184 | tf_op jit(solution)/shard_map/reduce_scatter | solution.py:200
  391.5 133.2 %all-gather.13.cloned.1.call-start = ((), (), s32[]{:S(2)}) async-start(), calls=%async_computation.12 | async-start | bytes 9437184 | tf_op jit(solution)/shard_map/all_gather | solution.py:210
  470.2 408.2 %reduce-scatter.17.cloned.1.call-start = ((), (), s32[]{:S(2)}) async-start(), calls=%async_computation.13 | async-start | bytes 9437184 | tf_op jit(solution)/shard_map/reduce_scatter | solution.py:265
  806.8 408.2 %all-reduce.5.cloned.1.call-start = ((), (), s32[]{:S(2)}) async-start(), calls=%async_computation.17 | async-start | bytes 19398656 | tf_op jit(solution)/shard_map/psum | solution.py:293
  849.5 439.5 %reduce-scatter.13.cloned.1.call-start = ((), (), s32[]{:S(2)}) async-start(), calls=%async_computation.9 | async-start | bytes 9437184 | tf_op jit(solution)/shard_map/reduce_scatter | solution.py:181
  860.7 465.4 %reduce-scatter.19.cloned.1.call-start = ((), (), s32[]{:S(2)}) async-start(), calls=%async_computation.15 | async-start | bytes 589824
  883.5 479.8 %reduce-scatter.21.cloned.1.call-start = ((), (), s32[]{:S(2)}) async-start(), calls=%async_computation.16 | async-start | bytes 589824
  884.7 698.2 %all-gather.15.cloned.1.call-start = ((), (), s32[]{:S(2)}) async-start(), calls=%async_computation.14 | async-start | bytes 15728640 | tf_op jit(solution)/shard_map/all_gather | solution.py:15
  1221.3 67.7 %copy-start.25 = (f32[1,2048]{1,0:T(1,128)S(1)}, f32[1,2048]{1,0:T(1,128)}, u32[]{:S(2)}) copy-start(f32[1,2048]{1,0:T(1,128)} %get-tuple-element.320) | copy-start | bytes 24580
  1221.3 67.7 %copy-start.29 = (f32[256]{0:T(256)S(1)}, f32[256]{0:T(256)}, u32[]{:S(2)}) copy-start(f32[256]{0:T(256)} %copy-done.28) | copy-start | bytes 3076
  1221.3 67.7 %copy-start.34 = (f32[256]{0:T(256)S(1)}, f32[256]{0:T(256)}, u32[]{:S(2)}) copy-start(f32[256]{0:T(256)} %copy-done.33) | copy-start | bytes 3076
  1221.3 67.7 %copy-start.39 = (f32[256]{0:T(256)S(1)}, f32[256]{0:T(256)}, u32[]{:S(2)}) copy-start(f32[256]{0:T(256)} %copy-done.38) | copy-start | bytes 3076
  1221.4 67.7 %copy-start.41 = (f32[256]{0:T(256)S(1)}, f32[256]{0:T(256)}, u32[]{:S(2)}) copy-start(f32[256]{0:T(256)} %copy-done.40) | copy-start | bytes 3076
  (54 other events, 322.6 us)
Sparse Core Ops, SparseCore 0:
  16.2 56.9 all-gather.6
  161.9 71.4 reduce-scatter.10
  239.3 54.2 all-gather.8
  295.3 54.2 all-gather.10
  391.6 71.4 reduce-scatter.14
  470.3 54.2 all-gather.12
  806.9 71.4 reduce-scatter.16
  881.9 333.1 all-reduce.4
  1218.5 70.4 reduce-scatter.12
  1291.9 34.0 reduce-scatter.18
  1329.2 34.0 reduce-scatter.20
  1364.7 218.1 all-gather.14
